TPU v7x, 8 devices: a whole 2x2x1 slice. The times are simulated.
8 devices in a mesh: dp: 2 (over y, z), tp: 4 (over x, core).
Axes of the slice: x: 2, y: 2, z: 1, core: 2. Of those that a mesh axis runs over, the one named last changes fastest.
Arguments:
- x: bfloat16 [128, 3072], P('dp'), parts along dimension 0
- k_cache: bfloat16 [128, 1024, 32, 96], P('dp', None, 'tp'), parts along dimension 0
- v_cache: bfloat16 [128, 1024, 32, 96], P('dp', None, 'tp'), parts along dimension 0
- gain_a: bfloat16 [3072], replicated
- wq: bfloat16 [3072, 3072], P(None, 'tp')
- wo: bfloat16 [3072, 3072], P('tp')
- gain_m: bfloat16 [3072], replicated
- w_gate: bfloat16 [3072, 8192], P(None, 'tp')
- w_up: bfloat16 [3072, 8192], P(None, 'tp')
- w_down: bfloat16 [8192, 3072], P('tp')
Outputs:
- output: bfloat16 [128, 3072], P('dp'), parts along dimension 0
There are 2 independent parts. A program takes and returns all parts, laid end to end along the dimension named above; an argument that names none is the same for every part.
All inputs are finite; a program needn't handle non-finite values.
Results may differ from a plain program's by a relative error of at most 0.017.
Values are sent between devices in bfloat16 or wider.
A program may use at most 2 GiB of HBM per device.

v0:
```python
import jax
import jax.numpy as jnp
from jax import lax
from jax.sharding import PartitionSpec as P

HEAD = 96
THETA = 10000


def normed(x, gain):
    wide = x.astype(jnp.float32)
    scale = lax.rsqrt(jnp.mean(wide * wide, -1, keepdims=True) + 1e-6)
    return (wide * scale * gain.astype(jnp.float32)).astype(jnp.bfloat16)


def turned(t, place, theta):
    half = t.shape[-1] // 2
    angle = place.astype(jnp.float32)[:, None] * theta ** (-jnp.arange(half, dtype=jnp.float32) / half)
    cos, sin = jnp.cos(angle)[:, None], jnp.sin(angle)[:, None]
    a, b = t[..., :half].astype(jnp.float32), t[..., half:].astype(jnp.float32)
    return jnp.concatenate([a * cos - b * sin, b * cos + a * sin], -1).astype(jnp.bfloat16)


def matmul(a, w):
    return jnp.dot(a, w, preferred_element_type=jnp.float32).astype(jnp.bfloat16)


def einsum(form, a, b):
    return jnp.einsum(form, a.astype(jnp.float32), b.astype(jnp.float32))


def seen_by(a, wq, k_cache, v_cache, head, theta):
    batch, cache, kv_heads = k_cache.shape[:3]
    place = jnp.full((batch,), cache - 1)
    q = turned(matmul(a, wq).reshape(batch, -1, head), place, theta).reshape(batch, kv_heads, -1, head)
    scores = einsum("bgsd,bugd->bgsu", q, k_cache) * head**-0.5
    weights = jax.nn.softmax(scores, -1).astype(jnp.bfloat16)
    return einsum("bgsu,bugd->bgsd", weights, v_cache).astype(jnp.bfloat16).reshape(batch, -1)


def hidden_of(b, w_gate, w_up):
    gate = jnp.dot(b, w_gate, preferred_element_type=jnp.float32)
    up = jnp.dot(b, w_up, preferred_element_type=jnp.float32)
    return (jax.nn.silu(gate) * up).astype(jnp.bfloat16)


def solution(mesh):
    def added(t, term):
        return (t.astype(jnp.float32) + lax.psum(term.astype(jnp.bfloat16), "tp").astype(jnp.float32)).astype(jnp.bfloat16)

    def step(x, k_cache, v_cache, gain_a, wq, wo, gain_m, w_gate, w_up, w_down):
        seen = seen_by(normed(x, gain_a), wq, k_cache, v_cache, HEAD, THETA)
        h = added(x, jnp.dot(seen, wo, preferred_element_type=jnp.float32))
        return added(h, jnp.dot(hidden_of(normed(h, gain_m), w_gate, w_up), w_down, preferred_element_type=jnp.float32))

    states, cache, columns, rows_of = P("dp", None), P("dp", None, "tp", None), P(None, "tp"), P("tp", None)
    return jax.shard_map(
        step,
        mesh=mesh,
        in_specs=(states, cache, cache, P(None), columns, rows_of, P(None), columns, columns, rows_of),
        out_specs=states,
        check_vma=False,
    )
```

profile of v0, /device:TPU:0, one launch (start us, length us, event | category | flops | bytes accessed | tf_op | source)
XLA Modules:
  0.0 175.0 jit_solution(17683409136684604359)
XLA Ops:
  6.5 0.0 all-reduce.3.cloned.1.call-start
  6.6 0.7 convert_element_type.66
  7.3 1.2 fusion.8
  8.5 3.5 %convolution_convert_fusion.2 = bf16[64,768]{1,0:T(8,128)(2,1)S(1)} fusion(bf16[3072,768]{1,0:T(8,128)(2,1)} %param.14, bf16[64,3072]{1,0:T(8,128)(2,1)} %param.10, f32[3072]{0:T(1024)S(1)} %convert_element_type.66, f32[64]{0:T(128)S(1)} %add_rsqrt_fusion.1), kind=kOutput, calls=%fused_computation.19 | convolution fusion | flops 302825472 | bytes 5222656 | tf_op jit(solution)/shard_map/dot_general | solution.py:25
  11.9 0.2 reshape.61
  12.1 0.1 fusion.25
  12.3 0.1 maximum_bitcast_fusion
  12.4 33.3 %fusion.28 = f32[64,8,1,1024]{3,2,1,0:T(1,128)S(1)} fusion(bf16[64,1024,8,96]{1,3,2,0:T(8,128)(2,1)} %param.11, bf16[64,8,96,1]{2,1,0,3:T(8,128)(2,1)S(1)} %maximum_bitcast_fusion), kind=kOutput, calls=%fused_computation.44 | convolution fusion | flops 100663296 | bytes 102858752 | tf_op jit(solution)/shard_map/bgsd,bugd->bgsu/dot_general | solution.py:29
  45.7 1.1 fusion.6
  46.8 36.4 %fusion.3 = f32[64,8,1,96]{3,2,1,0:T(1,128)S(1)} fusion(bf16[64,1024,8,96]{1,3,2,0:T(8,128)(2,1)} %param.12, bf16[64,8,1024,1]{2,1,0,3:T(8,128)(2,1)S(1)} %fusion.6), kind=kOutput, calls=%fused_computation.7 | convolution fusion | flops 100663296 | bytes 101908480 | tf_op jit(solution)/shard_map/bgsu,bugd->bgsd/dot_general | solution.py:29
  83.2 0.0 copy-start.1
  83.2 0.0 copy-start
  83.2 0.1 reshape.62
  83.4 4.0 %convolution_convert_fusion = bf16[64,3072]{1,0:T(8,128)(2,1)} fusion(bf16[64,768]{1,0:T(8,128)(2,1)S(1)} %reshape.62, bf16[768,3072]{1,0:T(8,128)(2,1)} %param.15), kind=kOutput, calls=%fused_computation.2 | convolution fusion | flops 302186496 | bytes 5210112 | tf_op jit(solution)/shard_map/dot_general | solution.py:53
  87.4 0.0 all-reduce.3.cloned.1.call-update
  87.4 0.2 all-reduce.5.cloned.1.call-start
  87.6 0.0 copy-done.1
  87.7 29.8 %all-reduce.3.cloned.1.call-done = bf16[64,3072]{1,0:T(8,128)(2,1)} async-done(((bf16[64,3072]{1,0:T(8,128)(2,1)}), bf16[64,3072]{1,0:T(8,128)(2,1)}) %all-reduce.3.cloned.1.call-update) | async-done | bytes 393232 | tf_op jit(solution)/shard_map/psum | solution.py:49
  117.5 1.2 fusion.12
  118.7 6.9 %fusion.33 = f32[64,2048]{1,0:T(8,128)S(1)} fusion(bf16[3072,2048]{1,0:T(8,128)(2,1)} %param.17, bf16[64,3072]{1,0:T(8,128)(2,1)S(1)} %get-tuple-element.6, f32[3072]{0:T(1024)S(1)} %convert_element_type.77, f32[64]{0:T(128)S(1)} %add_rsqrt_fusion), kind=kOutput, calls=%fused_computation.48 | convolution fusion | flops 806092800 | bytes 13512960 | tf_op jit(solution)/shard_map/dot_general | solution.py:42
  125.7 13.4 %convolution_convert_fusion.1 = bf16[64,3072]{1,0:T(8,128)(2,1)} fusion(bf16[2048,3072]{1,0:T(8,128)(2,1)} %param.19, bf16[3072,2048]{1,0:T(8,128)(2,1)} %param.18, f32[64,2048]{1,0:T(8,128)S(1)} %fusion.33, bf16[64,3072]{1,0:T(8,128)(2,1)S(1)} %get-tuple-element.6, f32[3072]{0:T(1024)S(1)} %convert_element_type.77, f32[64]{0:T(128)S(1)} %add_rsqrt_fusion), kind=kOutput, calls=%fused_computation.3 | convolution fusion | flops 1612382208 | bytes 26489088 | tf_op jit(solution)/shard_map/dot_general | solution.py:54
  139.1 0.0 all-reduce.5.cloned.1.call-update
  139.1 27.2 %all-reduce.5.cloned.1.call-done = bf16[64,3072]{1,0:T(8,128)(2,1)} async-done(((bf16[64,3072]{1,0:T(8,128)(2,1)}), bf16[64,3072]{1,0:T(8,128)(2,1)}) %all-reduce.5.cloned.1.call-update) | async-done | bytes 393232 | tf_op jit(solution)/shard_map/psum | solution.py:49
  166.4 1.8 %fusion.15 = bf16[64,3072]{1,0:T(8,128)(2,1)} fusion(bf16[64,3072]{1,0:T(8,128)(2,1)S(1)} %get-tuple-element.6, bf16[64,3072]{1,0:T(8,128)(2,1)} %all-reduce.5.cloned.1.call-done), kind=kLoop, calls=%fused_computation.28 | loop fusion | flops 786432 | bytes 1179648 | tf_op jit(solution)/shard_map/convert_element_type | solution.py:49
  (6 shorter events, 0.1 us)
Async XLA Ops:
  6.5 110.9 %all-reduce.3.cloned.1.call-start = ((), (), s32[]{:S(2)}) async-start(), calls=%async_computation | async-start | bytes 786432 | tf_op jit(solution)/shard_map/psum | solution.py:49
  83.2 4.5 %copy-start.1 = (bf16[3072]{0:T(1024)(128)(2,1)S(1)}, bf16[3072]{0:T(1024)(128)(2,1)}, u32[]{:S(2)}) copy-start(bf16[3072]{0:T(1024)(128)(2,1)} %param.16) | copy-start | bytes 18436
  83.2 34.3 %copy-start = (bf16[64,3072]{1,0:T(8,128)(2,1)S(1)}, bf16[64,3072]{1,0:T(8,128)(2,1)}, u32[]{:S(2)}) copy-start(bf16[64,3072]{1,0:T(8,128)(2,1)} %param.10) | copy-start | bytes 1179652
  87.4 79.0 %all-reduce.5.cloned.1.call-start = ((), (), s32[]{:S(2)}) async-start(), calls=%async_computation.1 | async-start | bytes 786432 | tf_op jit(solution)/shard_map/psum | solution.py:49
Sparse Core Ops, SparseCore 0:
  87.5 29.8 all-reduce.2
  139.3 27.0 all-reduce.4
where the time goes:
time: 175 us
  matrix products  97.5 us (56%)
  waiting for transfers between devices  57.1 us (33%)
  between operations  13.5 us (8%)
  other arithmetic  6.4 us (4%)
    dot_general x2, matrix products, einsum(): return jnp.einsum(form, a.astype(jnp.float32), b.astype(jnp.float32))  69.7 us
    psum x2, waiting for transfers between devices, added(): lax.psum(term.astype(jnp.bfloat16), 'tp').astype(jnp.float32)  57 us
    dot_general x1, matrix products, step(): jnp.dot(hidden_of(normed(h, gain_m), w_gate, w_up), w_down, preferred_ele...  13.4 us
    dot_general x1, matrix products, hidden_of(): gate = jnp.dot(b, w_gate, preferred_element_type=jnp.float32)  6.94 us
    dot_general x1, matrix products, step(): h = added(x, jnp.dot(seen, wo, preferred_element_type=jnp.float32))  4.02 us
  transfers between devices with their start and end apart: 2, of which 2 were waited for; matrix products, arithmetic and copies ran while one was open for 0% of the time, Pallas kernels for 0%

commit v1 on v0

v1 whole, which is shorter than its diff:
```python
import jax
import jax.numpy as jnp
import numpy as np
from jax import lax
from jax.experimental import pallas as pl
from jax.experimental.pallas import tpu as pltpu
from jax.sharding import PartitionSpec as P

HEAD = 96
THETA = 10000
EPS = 1e-6
SEQS = 2
SLOTS = 3
GROUP = 16
FCHUNK = 512
DCHUNK = 512

F32, BF16 = jnp.float32, jnp.bfloat16
NT = (((1,), (1,)), ((), ()))


def rotary_table(heads, head, place):
    half = head // 2
    angle = np.float32(place) * np.float32(THETA) ** (-np.arange(half, dtype=np.float32) / np.float32(half))
    cos, sin, zero = np.cos(angle), np.sin(angle), np.zeros(half, np.float32)
    rows = [np.concatenate(r) for r in ((cos, cos), (-sin, zero), (zero, sin))]
    return np.stack([np.tile(r, heads) for r in rows]).astype(np.float32)


def dot(a, b):
    return jnp.dot(a, b, preferred_element_type=F32)


def normed(wide, gain):
    scale = lax.rsqrt(jnp.mean(wide * wide, -1, keepdims=True) + EPS)
    return (wide * scale * gain).astype(BF16)


def layer_kernel(
    x_hbm, k_hbm, v_hbm, ga_hbm, wq_hbm, wo_hbm, gm_hbm, wg_hbm, wu_hbm, wd_hbm, trig_hbm,
    y_ref,
    k_buf, v_buf, wg, wu, wd, wo, x, ga, gm, trig,
    q, o, term, send1, recv1, send2, recv2, h, hid,
    send3, recv3, send4, recv4,
    ksem, vsem, wsem, gsem, usem, dsem, isem,
    s1, r1, s2, r2, s3, r3, s4, r4, s5, r5, s6, r6,
):
    rows, d = x.shape
    width = q.shape[1]
    ff = hid.shape[1]
    half = d // 2
    heads = width // HEAD
    t = lax.axis_index("tp")
    core = lax.rem(t, 2)
    other = 1 - core
    partner = t + 1 - 2 * core
    across = lax.rem(t + 2, 4)
    blocks = rows // SEQS
    per_group = GROUP // SEQS
    groups = rows // GROUP
    nf, nd = ff // FCHUNK, d // DCHUNK
    dh = DCHUNK // 2

    barrier = pltpu.get_barrier_semaphore()
    for peer in (partner, across):
        pl.semaphore_signal(barrier, inc=1, device_id={"tp": peer}, device_id_type=pl.DeviceIdType.MESH)

    def cache_copies(b, slot):
        at = pl.ds(b * SEQS, SEQS)
        return (
            pltpu.make_async_copy(k_hbm.at[at], k_buf.at[slot], ksem.at[slot]),
            pltpu.make_async_copy(v_hbm.at[at], v_buf.at[slot], vsem.at[slot]),
        )

    wq = wg.at[:, pl.ds(0, width)]
    first = [
        pltpu.make_async_copy(x_hbm, x, isem.at[0]),
        pltpu.make_async_copy(ga_hbm, ga, isem.at[1]),
        pltpu.make_async_copy(trig_hbm, trig, isem.at[2]),
        pltpu.make_async_copy(wq_hbm, wq, isem.at[3]),
    ]
    later = [
        pltpu.make_async_copy(gm_hbm, gm, isem.at[4]),
        pltpu.make_async_copy(wo_hbm, wo, wsem),
    ]
    gate_copy = [
        pltpu.make_async_copy(wg_hbm.at[:, pl.ds(c * FCHUNK, FCHUNK)], wg.at[:, pl.ds(c * FCHUNK, FCHUNK)], gsem.at[c])
        for c in range(nf)
    ]
    up_copy = [
        pltpu.make_async_copy(wu_hbm.at[:, pl.ds(c * FCHUNK, FCHUNK)], wu.at[:, pl.ds(c * FCHUNK, FCHUNK)], usem.at[c])
        for c in range(nf)
    ]
    down_copy = [
        pltpu.make_async_copy(wd_hbm.at[:, pl.ds(c * DCHUNK, DCHUNK)], wd.at[:, pl.ds(c * DCHUNK, DCHUNK)], dsem.at[c])
        for c in range(nd)
    ]

    for c in first:
        c.start()
    for s in range(SLOTS):
        for c in cache_copies(s, s):
            c.start()
    for c in later:
        c.start()

    for c in first[:3]:
        c.wait()
    a = normed(x[...].astype(F32), ga[...].astype(F32))
    first[3].wait()
    q0 = dot(a, wq[...]).astype(BF16).astype(F32)
    ahead = pltpu.roll(q0, width - HEAD // 2, 1)
    behind = pltpu.roll(q0, HEAD // 2, 1)
    q[...] = (q0 * trig[0:1, :] + ahead * trig[1:2, :] + behind * trig[2:3, :]).astype(BF16).astype(F32)

    lane = lax.broadcasted_iota(jnp.int32, (heads, width), 1)
    top = lax.broadcasted_iota(jnp.int32, (heads, width), 0) * HEAD
    own_head = (lane >= top) & (lane < top + HEAD)

    pl.semaphore_wait(barrier, 2)

    def to(peer, src, dst, ssem, rsem):
        return pltpu.make_async_remote_copy(
            src_ref=src, dst_ref=dst, send_sem=ssem, recv_sem=rsem,
            device_id={"tp": peer}, device_id_type=pl.DeviceIdType.MESH,
        )

    mine = pl.ds(pl.multiple_of(core * half, half), half)
    theirs = pl.ds(pl.multiple_of(other * half, half), half)

    def rows_of(g):
        return pl.ds(pl.multiple_of(g * GROUP, GROUP), GROUP)

    def copy1(g):
        return to(partner, send1.at[rows_of(g)], recv1.at[rows_of(g)], s1.at[g], r1.at[g])

    def copy2(g):
        return to(across, send2.at[rows_of(g)], recv2.at[rows_of(g)], s2.at[g], r2.at[g])

    def copy3(g):
        return to(partner, h.at[rows_of(g), mine], h.at[rows_of(g), mine], s3.at[g], r3.at[g])

    def project(g):
        at = rows_of(g)
        seen = o[at, :].astype(BF16)
        send1[at, :] = dot(seen, wo[:, theirs]).astype(BF16)
        copy1(g).start()
        term[at, :] = dot(seen, wo[:, mine])

    def pair_sum(g):
        at = rows_of(g)
        copy1(g).wait_recv()
        send2[at, :] = (term[at, :] + recv1[at, :].astype(F32)).astype(BF16)
        copy2(g).start()

    def finish(g):
        at = rows_of(g)
        copy2(g).wait_recv()
        total = send2[at, :].astype(F32) + recv2[at, :].astype(F32)
        h[at, mine] = (x[at, mine].astype(F32) + total).astype(BF16)
        copy3(g).start()

    def softmax(scores):
        scores = scores * HEAD**-0.5
        e = jnp.exp(scores - jnp.max(scores, -1, keepdims=True))
        return (e / jnp.sum(e, -1, keepdims=True)).astype(BF16)

    later[1].wait()

    def block(b, carry):
        slot = lax.rem(b, SLOTS)
        kc, vc = cache_copies(b, slot)
        kc.wait()
        vc.wait()
        scores = []
        for i in range(SEQS):
            row = q[pl.ds(b * SEQS + i, 1), :]
            spread = jnp.where(own_head, jnp.broadcast_to(row, (heads, width)), 0.0).astype(BF16)
            scores.append(dot(spread, k_buf[slot, i]))
        for i in range(SEQS):
            weights = softmax(scores[i])
            out = lax.dot_general(weights, v_buf[slot, i], NT, preferred_element_type=F32)
            o[pl.ds(b * SEQS + i, 1), :] = jnp.sum(jnp.where(own_head, out, 0.0), 0, keepdims=True)

        @pl.when(b + SLOTS < blocks)
        def _():
            for c in cache_copies(b + SLOTS, slot):
                c.start()

        for n in range(SLOTS):
            @pl.when(b == blocks - SLOTS + n)
            def _():
                gate_copy[n].start()
                up_copy[n].start()

        g = lax.div(b, per_group)
        step = lax.rem(b, per_group)

        @pl.when(step == per_group - 1)
        def _():
            project(g)

        @pl.when((step == 0) & (b > 0))
        def _():
            pair_sum(g - 1)

        @pl.when((step == 3) & (b > per_group))
        def _():
            finish(g - 1)

        return carry

    lax.fori_loop(0, blocks, block, 0)
    for n in range(SLOTS, nf):
        gate_copy[n].start()
        up_copy[n].start()
    for c in down_copy:
        c.start()

    pair_sum(groups - 1)
    finish(groups - 1)
    later[0].wait()
    for g in range(groups):
        copy3(g).wait_recv()
    b_states = normed(h[...].astype(F32), gm[...].astype(F32))

    for n in range(nf):
        at = pl.ds(n * FCHUNK, FCHUNK)
        gate_copy[n].wait()
        gate = dot(b_states, wg[:, at])
        up_copy[n].wait()
        up = dot(b_states, wu[:, at])
        hid[:, at] = (gate * jax.nn.sigmoid(gate) * up).astype(BF16)

    def columns(n, which):
        return pl.ds(pl.multiple_of(n * DCHUNK + which * dh, dh), dh)

    def part(n):
        return pl.ds(n * dh, dh)

    def copy4(n):
        return to(partner, send3.at[:, part(n)], recv3.at[:, part(n)], s4.at[n], r4.at[n])

    def copy5(n):
        return to(across, send4.at[:, part(n)], recv4.at[:, part(n)], s5.at[n], r5.at[n])

    def copy6(n):
        return to(partner, y_ref.at[:, columns(n, core)], y_ref.at[:, columns(n, core)], s6.at[n], r6.at[n])

    term2 = term
    def down(n):
        down_copy[n].wait()
        send3[:, part(n)] = dot(hid[...], wd[:, columns(n, other)]).astype(BF16)
        copy4(n).start()
        term2[:, part(n)] = dot(hid[...], wd[:, columns(n, core)])

    def down_pair(n):
        copy4(n).wait_recv()
        send4[:, part(n)] = (term2[:, part(n)] + recv3[:, part(n)].astype(F32)).astype(BF16)
        copy5(n).start()

    def down_finish(n):
        copy5(n).wait_recv()
        total = send4[:, part(n)].astype(F32) + recv4[:, part(n)].astype(F32)
        y_ref[:, columns(n, core)] = (h[:, columns(n, core)].astype(F32) + total).astype(BF16)
        copy6(n).start()

    lag = 3
    for n in range(nd + lag):
        if n < nd:
            down(n)
        if n >= lag:
            down_pair(n - lag)
    for n in range(nd):
        down_finish(n)
    for g in range(groups):
        copy1(g).wait_send()
        copy2(g).wait_send()
        copy3(g).wait_send()
    for n in range(nd):
        copy4(n).wait_send()
        copy5(n).wait_send()
        copy6(n).wait()


def solution(mesh):
    def step(x, k_cache, v_cache, gain_a, wq, wo, gain_m, w_gate, w_up, w_down):
        rows, d = x.shape
        cache, heads = k_cache.shape[1:3]
        width = heads * HEAD
        ff = w_gate.shape[1]
        turned_cache = [c.transpose(0, 2, 3, 1).reshape(rows, width, cache) for c in (k_cache, v_cache)]
        trig = jnp.asarray(rotary_table(heads, HEAD, cache - 1))
        gains = [g.reshape(1, d) for g in (gain_a, gain_m)]
        half, groups, nf, nd = d // 2, rows // GROUP, ff // FCHUNK, d // DCHUNK
        dma = pltpu.SemaphoreType.DMA
        return pl.pallas_call(
            layer_kernel,
            out_shape=jax.ShapeDtypeStruct((rows, d), BF16),
            in_specs=[pl.BlockSpec(memory_space=pl.ANY)] * 11,
            out_specs=pl.BlockSpec(memory_space=pltpu.VMEM),
            scratch_shapes=[
                pltpu.VMEM((SLOTS, SEQS, width, cache), BF16),
                pltpu.VMEM((SLOTS, SEQS, width, cache), BF16),
                pltpu.VMEM((d, ff), BF16),
                pltpu.VMEM((d, ff), BF16),
                pltpu.VMEM((ff, d), BF16),
                pltpu.VMEM((width, d), BF16),
                pltpu.VMEM((rows, d), BF16),
                pltpu.VMEM((1, d), BF16),
                pltpu.VMEM((1, d), BF16),
                pltpu.VMEM((3, width), F32),
                pltpu.VMEM((rows, width), F32),
                pltpu.VMEM((rows, width), F32),
                pltpu.VMEM((rows, half), F32),
                pltpu.VMEM((rows, half), BF16),
                pltpu.VMEM((rows, half), BF16),
                pltpu.VMEM((rows, half), BF16),
                pltpu.VMEM((rows, half), BF16),
                pltpu.VMEM((rows, d), BF16),
                pltpu.VMEM((rows, ff), BF16),
                pltpu.VMEM((rows, half), BF16),
                pltpu.VMEM((rows, half), BF16),
                pltpu.VMEM((rows, half), BF16),
                pltpu.VMEM((rows, half), BF16),
                dma((SLOTS,)), dma((SLOTS,)), dma, dma((nf,)), dma((nf,)), dma((nd,)), dma((5,)),
                *[dma((groups,)) for _ in range(6)],
                *[dma((nd,)) for _ in range(6)],
            ],
            compiler_params=pltpu.CompilerParams(
                collective_id=0, has_side_effects=True, vmem_limit_bytes=67043328
            ),
            name="decode_layer",
        )(x, *turned_cache, gains[0], wq, wo, gains[1], w_gate, w_up, w_down, trig)

    states, cache, columns, rows_of = P("dp", None), P("dp", None, "tp", None), P(None, "tp"), P("tp", None)
    return jax.shard_map(
        step,
        mesh=mesh,
        in_specs=(states, cache, cache, P(None), columns, rows_of, P(None), columns, columns, rows_of),
        out_specs=states,
        check_vma=False,
    )
```

time: 175 us -> 93.8 us (0.54)
  matrix products: 97.5 us -> 0 us
  Pallas kernels: 0 us -> 89.2 us
  waiting for transfers between devices: 57.1 us -> 0 us
  between operations: 13.5 us -> 0.01 us
  other arithmetic: 6.4 us -> 0 us
  local copies, waits for them, and re-layouts: 0.3 us -> 4.36 us
    dot_general x6 -> x0, matrix products: 97.5 us -> none  [the longest x2 69.7 us: einsum(): return jnp.einsum(form, a.astype(jnp.float32), b.astype(jnp.float32))]
    pallas_call x0 -> x1, Pallas kernels: none -> 89.2 us  [step(): pl.pallas_call(layer_kernel, out_shape=jax.ShapeDtypeStruct((rows, d), BF...]
    psum x2 -> x0, waiting for transfers between devices: 57 us -> none  [added(): lax.psum(term.astype(jnp.bfloat16), 'tp').astype(jnp.float32)]
    convert_element_type x4 -> x0, other arithmetic: 2.55 us -> none  [the longest x1 1.83 us: added(): (t.astype(jnp.float32) + lax.psum(term.astype(jnp.bfloat16), 'tp').astype...]
    reduce_sum x2 -> x0, other arithmetic: 2.41 us -> none  [normed(): scale = lax.rsqrt(jnp.mean(wide * wide, -1, keepdims=True) + 1e-06)]
    reshape x2, local copies, waits for them, and re-layouts: 0.29 us -> 2.59 us  [step(): gains = [g.reshape(1, d) for g in (gain_a, gain_m)]]
    unnamed x4 -> x1, local copies, waits for them, and re-layouts: 0.01 us -> 1.77 us
  transfers between devices with their start and end apart: 2 -> 0, of which waited for: 2 -> 0; matrix products, arithmetic and copies ran while one was open for 0% -> 0% of each run, Pallas kernels for 0% -> 0%
where the time goes in v1:
time: 93.8 us; the launch traced here: 93.6 us
  Pallas kernels  89.2 us (95%)
  local copies, waits for them, and re-layouts  4.36 us (5%)
    pallas_call x1, Pallas kernels, step(): pl.pallas_call(layer_kernel, out_shape=jax.ShapeDtypeStruct((rows, d), BF...  89.2 us
    reshape x2, local copies, waits for them, and re-layouts, step(): gains = [g.reshape(1, d) for g in (gain_a, gain_m)]  2.59 us

profile of v1, /device:TPU:0, one launch (start us, length us, event | category | flops | bytes accessed | tf_op | source)
XLA Modules:
  0.0 93.6 jit_solution(16833591631570690089)
XLA Ops:
  0.0 1.3 %reshape.14.ga_hbm = bf16[1,3072]{1,0:T(2,128)(2,1)} reshape(bf16[3072]{0:T(1024)(128)(2,1)} %param.14) | data formatting | bytes 12288 | tf_op jit(solution)/shard_map/reshape | solution.py:294
  1.3 1.3 %reshape.15.gm_hbm = bf16[1,3072]{1,0:T(2,128)(2,1)} reshape(bf16[3072]{0:T(1024)(128)(2,1)} %param.17) | data formatting | bytes 12288 | tf_op jit(solution)/shard_map/reshape | solution.py:294
  2.6 89.2 %decode_layer.1 = bf16[64,3072]{1,0:T(8,128)(2,1)} custom-call(bf16[64,3072]{1,0:T(8,128)(2,1)} %x_hbm.1, bf16[64,768,1024]{2,1,0:T(8,128)(2,1)} %bitcast.1.k_hbm, bf16[64,768,1024]{2,1,0:T(8,128)(2,1)} %bitcast.3.v_hbm, bf16[1,3072]{1,0:T(2,128)(2,1)} %reshape.14.ga_hbm, bf16[3072,768]{1,0:T(8,128)(2,1)} %wq_hbm.1, bf16[768,3072]{1,0:T(8,128)(2,1)} %wo_hbm.1, ...), custom_call_target="tpu_custom_call" | custom-call | tf_op jit(solution)/shard_map/decode_layer/pallas_call | solution.py:297
  91.8 1.8 %copy.13 = bf16[64,3072]{1,0:T(8,128)(2,1)} copy(bf16[64,3072]{1,0:T(8,128)(2,1)} %decode_layer.1) | data formatting | bytes 786432

commit v2 on v1

--- a/solution.py
+++ b/solution.py
@@ -106,7 +106,8 @@
 
     for c in first[:3]:
         c.wait()
-    a = normed(x[...].astype(F32), ga[...].astype(F32))
+    with jax.named_scope('norm_a'):
+        a = normed(x[...].astype(F32), ga[...].astype(F32).reshape(1, d))
     first[3].wait()
     q0 = dot(a, wq[...]).astype(BF16).astype(F32)
     ahead = pltpu.roll(q0, width - HEAD // 2, 1)
@@ -170,8 +171,9 @@
     def block(b, carry):
         slot = lax.rem(b, SLOTS)
         kc, vc = cache_copies(b, slot)
-        kc.wait()
-        vc.wait()
+        with jax.named_scope('wait_cache'):
+            kc.wait()
+            vc.wait()
         scores = []
         for i in range(SEQS):
             row = q[pl.ds(b * SEQS + i, 1), :]
@@ -198,15 +200,18 @@
 
         @pl.when(step == per_group - 1)
         def _():
-            project(g)
+            with jax.named_scope('project'):
+                project(g)
 
         @pl.when((step == 0) & (b > 0))
         def _():
-            pair_sum(g - 1)
+            with jax.named_scope('pair_sum'):
+                pair_sum(g - 1)
 
         @pl.when((step == 3) & (b > per_group))
         def _():
-            finish(g - 1)
+            with jax.named_scope('finish'):
+                finish(g - 1)
 
         return carry
 
@@ -217,18 +222,24 @@
     for c in down_copy:
         c.start()
 
-    pair_sum(groups - 1)
-    finish(groups - 1)
+    with jax.named_scope('pair_sum'):
+        pair_sum(groups - 1)
+    with jax.named_scope('finish'):
+        finish(groups - 1)
     later[0].wait()
-    for g in range(groups):
-        copy3(g).wait_recv()
-    b_states = normed(h[...].astype(F32), gm[...].astype(F32))
+    with jax.named_scope('wait_h'):
+        for g in range(groups):
+            copy3(g).wait_recv()
+    with jax.named_scope('norm_m'):
+        b_states = normed(h[...].astype(F32), gm[...].astype(F32).reshape(1, d))
 
     for n in range(nf):
         at = pl.ds(n * FCHUNK, FCHUNK)
-        gate_copy[n].wait()
+        with jax.named_scope('wait_gate'):
+            gate_copy[n].wait()
         gate = dot(b_states, wg[:, at])
-        up_copy[n].wait()
+        with jax.named_scope('wait_up'):
+            up_copy[n].wait()
         up = dot(b_states, wu[:, at])
         hid[:, at] = (gate * jax.nn.sigmoid(gate) * up).astype(BF16)
 
@@ -268,11 +279,14 @@
     lag = 3
     for n in range(nd + lag):
         if n < nd:
-            down(n)
+            with jax.named_scope('down'):
+                down(n)
         if n >= lag:
-            down_pair(n - lag)
+            with jax.named_scope('down_pair'):
+                down_pair(n - lag)
     for n in range(nd):
-        down_finish(n)
+        with jax.named_scope('down_finish'):
+            down_finish(n)
     for g in range(groups):
         copy1(g).wait_send()
         copy2(g).wait_send()
@@ -291,7 +305,6 @@
         ff = w_gate.shape[1]
         turned_cache = [c.transpose(0, 2, 3, 1).reshape(rows, width, cache) for c in (k_cache, v_cache)]
         trig = jnp.asarray(rotary_table(heads, HEAD, cache - 1))
-        gains = [g.reshape(1, d) for g in (gain_a, gain_m)]
         half, groups, nf, nd = d // 2, rows // GROUP, ff // FCHUNK, d // DCHUNK
         dma = pltpu.SemaphoreType.DMA
         return pl.pallas_call(
@@ -307,8 +320,8 @@
                 pltpu.VMEM((ff, d), BF16),
                 pltpu.VMEM((width, d), BF16),
                 pltpu.VMEM((rows, d), BF16),
-                pltpu.VMEM((1, d), BF16),
-                pltpu.VMEM((1, d), BF16),
+                pltpu.VMEM((d,), BF16),
+                pltpu.VMEM((d,), BF16),
                 pltpu.VMEM((3, width), F32),
                 pltpu.VMEM((rows, width), F32),
                 pltpu.VMEM((rows, width), F32),
@@ -331,7 +344,7 @@
                 collective_id=0, has_side_effects=True, vmem_limit_bytes=67043328
             ),
             name="decode_layer",
-        )(x, *turned_cache, gains[0], wq, wo, gains[1], w_gate, w_up, w_down, trig)
+        )(x, *turned_cache, gain_a, wq, wo, gain_m, w_gate, w_up, w_down, trig)
 
     states, cache, columns, rows_of = P("dp", None), P("dp", None, "tp", None), P(None, "tp"), P("tp", None)
     return jax.shard_map(

time: 93.8 us -> 91.1 us (0.971)
  local copies, waits for them, and re-layouts: 4.36 us -> 1.77 us
    reshape x2 -> x0, local copies, waits for them, and re-layouts: 2.59 us -> none  [step(): gains = [g.reshape(1, d) for g in (gain_a, gain_m)]]
where the time goes in v2:
time: 91.1 us; the launch traced here: 91 us
  Pallas kernels  89.2 us (98%)
  local copies, waits for them, and re-layouts  1.77 us (2%)
    pallas_call x1, Pallas kernels, step(): pl.pallas_call(layer_kernel, out_shape=jax.ShapeDtypeStruct((rows, d), BF...  89.2 us

profile of v2, /device:TPU:0, one launch (start us, length us, event | category | flops | bytes accessed | tf_op | source)
XLA Modules:
  0.0 91.0 jit_solution(1212558280214309157)
XLA Ops:
  0.0 89.2 %decode_layer.1 = bf16[64,3072]{1,0:T(8,128)(2,1)} custom-call(bf16[64,3072]{1,0:T(8,128)(2,1)} %x_hbm.1, bf16[64,768,1024]{2,1,0:T(8,128)(2,1)} %bitcast.1.k_hbm, bf16[64,768,1024]{2,1,0:T(8,128)(2,1)} %bitcast.3.v_hbm, bf16[3072]{0:T(1024)(128)(2,1)} %ga_hbm.1, bf16[3072,768]{1,0:T(8,128)(2,1)} %wq_hbm.1, bf16[768,3072]{1,0:T(8,128)(2,1)} %wo_hbm.1, ...), custom_call_target="tpu_custom_call" | custom-call | tf_op jit(solution)/shard_map/decode_layer/pallas_call | solution.py:310
  89.2 1.8 %copy.13 = bf16[64,3072]{1,0:T(8,128)(2,1)} copy(bf16[64,3072]{1,0:T(8,128)(2,1)} %decode_layer.1) | data formatting | bytes 786432

commit v3 on v2

--- a/solution.py
+++ b/solution.py
@@ -12,8 +12,10 @@
 SEQS = 2
 SLOTS = 3
 GROUP = 16
+QCHUNK = 768
 FCHUNK = 512
 DCHUNK = 512
+LAG = 2
 
 F32, BF16 = jnp.float32, jnp.bfloat16
 NT = (((1,), (1,)), ((), ()))
@@ -41,8 +43,8 @@
     y_ref,
     k_buf, v_buf, wg, wu, wd, wo, x, ga, gm, trig,
     q, o, term, send1, recv1, send2, recv2, h, hid,
-    send3, recv3, send4, recv4,
-    ksem, vsem, wsem, gsem, usem, dsem, isem,
+    send3, recv3, send4, recv4, states, piece,
+    ksem, vsem, qsem, wsem, gsem, usem, dsem, isem,
     s1, r1, s2, r2, s3, r3, s4, r4, s5, r5, s6, r6,
 ):
     rows, d = x.shape
@@ -58,7 +60,7 @@
     blocks = rows // SEQS
     per_group = GROUP // SEQS
     groups = rows // GROUP
-    nf, nd = ff // FCHUNK, d // DCHUNK
+    nq, nf, nd = d // QCHUNK, ff // FCHUNK, d // DCHUNK
     dh = DCHUNK // 2
 
     barrier = pltpu.get_barrier_semaphore()
@@ -77,39 +79,57 @@
         pltpu.make_async_copy(x_hbm, x, isem.at[0]),
         pltpu.make_async_copy(ga_hbm, ga, isem.at[1]),
         pltpu.make_async_copy(trig_hbm, trig, isem.at[2]),
-        pltpu.make_async_copy(wq_hbm, wq, isem.at[3]),
+    ]
+    query_copy = [
+        pltpu.make_async_copy(wq_hbm.at[pl.ds(c * QCHUNK, QCHUNK)], wq.at[pl.ds(c * QCHUNK, QCHUNK)], qsem.at[c])
+        for c in range(nq)
     ]
     later = [
-        pltpu.make_async_copy(gm_hbm, gm, isem.at[4]),
+        pltpu.make_async_copy(gm_hbm, gm, isem.at[3]),
         pltpu.make_async_copy(wo_hbm, wo, wsem),
     ]
-    gate_copy = [
-        pltpu.make_async_copy(wg_hbm.at[:, pl.ds(c * FCHUNK, FCHUNK)], wg.at[:, pl.ds(c * FCHUNK, FCHUNK)], gsem.at[c])
-        for c in range(nf)
-    ]
-    up_copy = [
-        pltpu.make_async_copy(wu_hbm.at[:, pl.ds(c * FCHUNK, FCHUNK)], wu.at[:, pl.ds(c * FCHUNK, FCHUNK)], usem.at[c])
-        for c in range(nf)
-    ]
-    down_copy = [
-        pltpu.make_async_copy(wd_hbm.at[:, pl.ds(c * DCHUNK, DCHUNK)], wd.at[:, pl.ds(c * DCHUNK, DCHUNK)], dsem.at[c])
-        for c in range(nd)
-    ]
-
-    for c in first:
+
+    def hidden_units(n):
+        return pl.ds(pl.multiple_of(n * FCHUNK, FCHUNK), FCHUNK)
+
+    def out_columns(n):
+        return pl.ds(pl.multiple_of(n * DCHUNK, DCHUNK), DCHUNK)
+
+    def gate_copy(n):
+        return pltpu.make_async_copy(wg_hbm.at[:, hidden_units(n)], wg.at[:, hidden_units(n)], gsem.at[n])
+
+    def up_copy(n):
+        return pltpu.make_async_copy(wu_hbm.at[:, hidden_units(n)], wu.at[:, hidden_units(n)], usem.at[n])
+
+    def down_copy(n):
+        return pltpu.make_async_copy(wd_hbm.at[:, out_columns(n)], wd.at[:, out_columns(n)], dsem.at[n])
+
+    for c in first + query_copy:
         c.start()
-    for s in range(SLOTS):
+    for c in cache_copies(0, 0):
+        c.start()
+
+    for c in first[:3]:
+        c.wait()
+    with jax.named_scope('norm_a'):
+        a = normed(x[...].astype(F32), ga[...].astype(F32).reshape(1, d))
+        states[...] = a
+    for c in cache_copies(1, 1):
+        c.start()
+    for n in range(nq):
+        with jax.named_scope('wait_wq'):
+            query_copy[n].wait()
+        part_q = dot(states[:, n * QCHUNK:(n + 1) * QCHUNK], wg[n * QCHUNK:(n + 1) * QCHUNK, 0:width])
+        if n == 0:
+            q[...] = part_q
+        else:
+            q[...] += part_q
+    for s in range(2, SLOTS):
         for c in cache_copies(s, s):
             c.start()
     for c in later:
         c.start()
-
-    for c in first[:3]:
-        c.wait()
-    with jax.named_scope('norm_a'):
-        a = normed(x[...].astype(F32), ga[...].astype(F32).reshape(1, d))
-    first[3].wait()
-    q0 = dot(a, wq[...]).astype(BF16).astype(F32)
+    q0 = q[...].astype(BF16).astype(F32)
     ahead = pltpu.roll(q0, width - HEAD // 2, 1)
     behind = pltpu.roll(q0, HEAD // 2, 1)
     q[...] = (q0 * trig[0:1, :] + ahead * trig[1:2, :] + behind * trig[2:3, :]).astype(BF16).astype(F32)
@@ -165,8 +185,6 @@
         scores = scores * HEAD**-0.5
         e = jnp.exp(scores - jnp.max(scores, -1, keepdims=True))
         return (e / jnp.sum(e, -1, keepdims=True)).astype(BF16)
-
-    later[1].wait()
 
     def block(b, carry):
         slot = lax.rem(b, SLOTS)
@@ -192,12 +210,16 @@
         for n in range(SLOTS):
             @pl.when(b == blocks - SLOTS + n)
             def _():
-                gate_copy[n].start()
-                up_copy[n].start()
+                gate_copy(n).start()
+                up_copy(n).start()
 
         g = lax.div(b, per_group)
         step = lax.rem(b, per_group)
 
+        @pl.when(b == per_group - 1)
+        def _():
+            later[1].wait()
+
         @pl.when(step == per_group - 1)
         def _():
             with jax.named_scope('project'):
@@ -217,10 +239,8 @@
 
     lax.fori_loop(0, blocks, block, 0)
     for n in range(SLOTS, nf):
-        gate_copy[n].start()
-        up_copy[n].start()
-    for c in down_copy:
-        c.start()
+        gate_copy(n).start()
+        up_copy(n).start()
 
     with jax.named_scope('pair_sum'):
         pair_sum(groups - 1)
@@ -230,24 +250,28 @@
     with jax.named_scope('wait_h'):
         for g in range(groups):
             copy3(g).wait_recv()
+    for n in range(nd):
+        down_copy(n).start()
     with jax.named_scope('norm_m'):
-        b_states = normed(h[...].astype(F32), gm[...].astype(F32).reshape(1, d))
-
-    for n in range(nf):
-        at = pl.ds(n * FCHUNK, FCHUNK)
-        with jax.named_scope('wait_gate'):
-            gate_copy[n].wait()
-        gate = dot(b_states, wg[:, at])
-        with jax.named_scope('wait_up'):
-            up_copy[n].wait()
-        up = dot(b_states, wu[:, at])
+        states[...] = normed(h[...].astype(F32), gm[...].astype(F32).reshape(1, d))
+
+    def gate_up(n, carry):
+        at = hidden_units(n)
+        with jax.named_scope('wait_gate_up'):
+            gate_copy(n).wait()
+            up_copy(n).wait()
+        gate = dot(states[...], wg[:, at])
+        up = dot(states[...], wu[:, at])
         hid[:, at] = (gate * jax.nn.sigmoid(gate) * up).astype(BF16)
+        return carry
+
+    lax.fori_loop(0, nf, gate_up, 0)
 
     def columns(n, which):
         return pl.ds(pl.multiple_of(n * DCHUNK + which * dh, dh), dh)
 
     def part(n):
-        return pl.ds(n * dh, dh)
+        return pl.ds(pl.multiple_of(n * dh, dh), dh)
 
     def copy4(n):
         return to(partner, send3.at[:, part(n)], recv3.at[:, part(n)], s4.at[n], r4.at[n])
@@ -258,43 +282,50 @@
     def copy6(n):
         return to(partner, y_ref.at[:, columns(n, core)], y_ref.at[:, columns(n, core)], s6.at[n], r6.at[n])
 
-    term2 = term
     def down(n):
-        down_copy[n].wait()
-        send3[:, part(n)] = dot(hid[...], wd[:, columns(n, other)]).astype(BF16)
+        with jax.named_scope('wait_down'):
+            down_copy(n).wait()
+        piece[...] = dot(hid[...], wd[:, out_columns(n)])
+        send3[:, part(n)] = piece[:, pl.ds(pl.multiple_of(other * dh, dh), dh)].astype(BF16)
         copy4(n).start()
-        term2[:, part(n)] = dot(hid[...], wd[:, columns(n, core)])
+        term[:, part(n)] = piece[:, pl.ds(pl.multiple_of(core * dh, dh), dh)]
 
     def down_pair(n):
-        copy4(n).wait_recv()
-        send4[:, part(n)] = (term2[:, part(n)] + recv3[:, part(n)].astype(F32)).astype(BF16)
+        with jax.named_scope('wait_pair'):
+            copy4(n).wait_recv()
+        send4[:, part(n)] = (term[:, part(n)] + recv3[:, part(n)].astype(F32)).astype(BF16)
         copy5(n).start()
 
-    def down_finish(n):
-        copy5(n).wait_recv()
+    def down_finish(n, carry):
+        with jax.named_scope('wait_across'):
+            copy5(n).wait_recv()
         total = send4[:, part(n)].astype(F32) + recv4[:, part(n)].astype(F32)
         y_ref[:, columns(n, core)] = (h[:, columns(n, core)].astype(F32) + total).astype(BF16)
         copy6(n).start()
-
-    lag = 3
-    for n in range(nd + lag):
-        if n < nd:
-            with jax.named_scope('down'):
-                down(n)
-        if n >= lag:
-            with jax.named_scope('down_pair'):
-                down_pair(n - lag)
-    for n in range(nd):
-        with jax.named_scope('down_finish'):
-            down_finish(n)
-    for g in range(groups):
-        copy1(g).wait_send()
-        copy2(g).wait_send()
-        copy3(g).wait_send()
-    for n in range(nd):
-        copy4(n).wait_send()
-        copy5(n).wait_send()
-        copy6(n).wait()
+        return carry
+
+    def down_step(n, carry):
+        @pl.when(n < nd)
+        def _():
+            down(n)
+
+        @pl.when(n >= LAG)
+        def _():
+            down_pair(n - LAG)
+
+        return carry
+
+    lax.fori_loop(0, nd + LAG, down_step, 0)
+    lax.fori_loop(0, nd, down_finish, 0)
+    with jax.named_scope('last_waits'):
+        for g in range(groups):
+            copy1(g).wait_send()
+            copy2(g).wait_send()
+            copy3(g).wait_send()
+        for n in range(nd):
+            copy4(n).wait_send()
+            copy5(n).wait_send()
+            copy6(n).wait()
 
 
 def solution(mesh):
@@ -336,7 +367,9 @@
                 pltpu.VMEM((rows, half), BF16),
                 pltpu.VMEM((rows, half), BF16),
                 pltpu.VMEM((rows, half), BF16),
-                dma((SLOTS,)), dma((SLOTS,)), dma, dma((nf,)), dma((nf,)), dma((nd,)), dma((5,)),
+                pltpu.VMEM((rows, d), BF16),
+                pltpu.VMEM((rows, DCHUNK), F32),
+                dma((SLOTS,)), dma((SLOTS,)), dma((d // QCHUNK,)), dma, dma((nf,)), dma((nf,)), dma((nd,)), dma((4,)),
                 *[dma((groups,)) for _ in range(6)],
                 *[dma((nd,)) for _ in range(6)],
             ],

time: 91.1 us -> 86.9 us (0.954)
  Pallas kernels: 89.2 us -> 85 us
    pallas_call x1, Pallas kernels: 89.2 us -> 85 us  [step(): pl.pallas_call(layer_kernel, out_shape=jax.ShapeDtypeStruct((rows, d), BF...]
where the time goes in v3:
time: 86.9 us; the launch traced here: 86.7 us
  Pallas kernels  85 us (98%)
  local copies, waits for them, and re-layouts  1.77 us (2%)
    pallas_call x1, Pallas kernels, step(): pl.pallas_call(layer_kernel, out_shape=jax.ShapeDtypeStruct((rows, d), BF...  85 us
    unnamed x1, local copies, waits for them, and re-layouts  1.77 us

profile of v3, /device:TPU:0, one launch (start us, length us, event | category | flops | bytes accessed | tf_op | source)
XLA Modules:
  0.0 86.7 jit_solution(16030196062125526868)
XLA Ops:
  0.0 85.0 %decode_layer.1 = bf16[64,3072]{1,0:T(8,128)(2,1)} custom-call(bf16[64,3072]{1,0:T(8,128)(2,1)} %x_hbm.1, bf16[64,768,1024]{2,1,0:T(8,128)(2,1)} %bitcast.1.k_hbm, bf16[64,768,1024]{2,1,0:T(8,128)(2,1)} %bitcast.3.v_hbm, bf16[3072]{0:T(1024)(128)(2,1)} %ga_hbm.1, bf16[3072,768]{1,0:T(8,128)(2,1)} %wq_hbm.1, bf16[768,3072]{1,0:T(8,128)(2,1)} %wo_hbm.1, ...), custom_call_target="tpu_custom_call" | custom-call | tf_op jit(solution)/shard_map/decode_layer/pallas_call | solution.py:341
  85.0 1.8 %copy.13 = bf16[64,3072]{1,0:T(8,128)(2,1)} copy(bf16[64,3072]{1,0:T(8,128)(2,1)} %decode_layer.1) | data formatting | bytes 786432

commit v4 on v3

--- a/solution.py
+++ b/solution.py
@@ -9,11 +9,13 @@
 HEAD = 96
 THETA = 10000
 EPS = 1e-6
-SEQS = 2
-SLOTS = 3
+EARLY = 3
+SLOTS = 5
 GROUP = 16
 QCHUNK = 768
 FCHUNK = 512
+FSTEP = 1024
+PADDED = 128
 DCHUNK = 512
 LAG = 2
 
@@ -40,12 +42,12 @@
 
 def layer_kernel(
     x_hbm, k_hbm, v_hbm, ga_hbm, wq_hbm, wo_hbm, gm_hbm, wg_hbm, wu_hbm, wd_hbm, trig_hbm,
-    y_ref,
+    y_hbm,
     k_buf, v_buf, wg, wu, wd, wo, x, ga, gm, trig,
     q, o, term, send1, recv1, send2, recv2, h, hid,
-    send3, recv3, send4, recv4, states, piece,
+    send3, recv3, send4, recv4, states, piece, y_ref,
     ksem, vsem, qsem, wsem, gsem, usem, dsem, isem,
-    s1, r1, s2, r2, s3, r3, s4, r4, s5, r5, s6, r6,
+    s1, r1, s2, r2, s3, r3, s4, r4, s5, r5, s6, r6, ysem,
 ):
     rows, d = x.shape
     width = q.shape[1]
@@ -57,8 +59,6 @@
     other = 1 - core
     partner = t + 1 - 2 * core
     across = lax.rem(t + 2, 4)
-    blocks = rows // SEQS
-    per_group = GROUP // SEQS
     groups = rows // GROUP
     nq, nf, nd = d // QCHUNK, ff // FCHUNK, d // DCHUNK
     dh = DCHUNK // 2
@@ -67,12 +67,13 @@
     for peer in (partner, across):
         pl.semaphore_signal(barrier, inc=1, device_id={"tp": peer}, device_id_type=pl.DeviceIdType.MESH)
 
-    def cache_copies(b, slot):
-        at = pl.ds(b * SEQS, SEQS)
-        return (
-            pltpu.make_async_copy(k_hbm.at[at], k_buf.at[slot], ksem.at[slot]),
-            pltpu.make_async_copy(v_hbm.at[at], v_buf.at[slot], vsem.at[slot]),
-        )
+    def key_copy(i):
+        slot = lax.rem(i, SLOTS)
+        return pltpu.make_async_copy(k_hbm.at[i], k_buf.at[slot], ksem.at[slot])
+
+    def value_copy(i):
+        slot = lax.rem(i, SLOTS)
+        return pltpu.make_async_copy(v_hbm.at[i], v_buf.at[slot], vsem.at[slot])
 
     wq = wg.at[:, pl.ds(0, width)]
     first = [
@@ -101,32 +102,38 @@
     def up_copy(n):
         return pltpu.make_async_copy(wu_hbm.at[:, hidden_units(n)], wu.at[:, hidden_units(n)], usem.at[n])
 
+    def weight_copy(n):
+        return (up_copy if n % 2 else gate_copy)(n // 2)
+
     def down_copy(n):
         return pltpu.make_async_copy(wd_hbm.at[:, out_columns(n)], wd.at[:, out_columns(n)], dsem.at[n])
 
     for c in first + query_copy:
         c.start()
-    for c in cache_copies(0, 0):
-        c.start()
+    for i in range(2):
+        key_copy(i).start()
+        value_copy(i).start()
 
     for c in first[:3]:
         c.wait()
     with jax.named_scope('norm_a'):
         a = normed(x[...].astype(F32), ga[...].astype(F32).reshape(1, d))
-        states[...] = a
-    for c in cache_copies(1, 1):
-        c.start()
+        states[0:rows, :] = a
+        states[rows:PADDED, :] = jnp.zeros((PADDED - rows, d), BF16)
+    for i in range(2, 4):
+        key_copy(i).start()
+        value_copy(i).start()
     for n in range(nq):
         with jax.named_scope('wait_wq'):
             query_copy[n].wait()
-        part_q = dot(states[:, n * QCHUNK:(n + 1) * QCHUNK], wg[n * QCHUNK:(n + 1) * QCHUNK, 0:width])
+        part_q = dot(states[0:rows, n * QCHUNK:(n + 1) * QCHUNK], wg[n * QCHUNK:(n + 1) * QCHUNK, 0:width])
         if n == 0:
             q[...] = part_q
         else:
             q[...] += part_q
-    for s in range(2, SLOTS):
-        for c in cache_copies(s, s):
-            c.start()
+    for i in range(4, SLOTS):
+        key_copy(i).start()
+        value_copy(i).start()
     for c in later:
         c.start()
     q0 = q[...].astype(BF16).astype(F32)
@@ -186,61 +193,72 @@
         e = jnp.exp(scores - jnp.max(scores, -1, keepdims=True))
         return (e / jnp.sum(e, -1, keepdims=True)).astype(BF16)
 
-    def block(b, carry):
-        slot = lax.rem(b, SLOTS)
-        kc, vc = cache_copies(b, slot)
+    def scores_of(i):
+        row = q[pl.ds(i, 1), :]
+        spread = jnp.where(own_head, jnp.broadcast_to(row, (heads, width)), 0.0).astype(BF16)
+        return dot(spread, k_buf[lax.rem(i, SLOTS)])
+
+    def add_values(i, weights):
+        out = lax.dot_general(weights, v_buf[lax.rem(i, SLOTS)], NT, preferred_element_type=F32)
+        o[pl.ds(i, 1), :] = jnp.sum(jnp.where(own_head, out, 0.0), 0, keepdims=True)
+
+    key_copy(0).wait()
+    weights = softmax(scores_of(0))
+    key_copy(SLOTS).start()
+
+    def sequence(i, weights):
         with jax.named_scope('wait_cache'):
-            kc.wait()
-            vc.wait()
-        scores = []
-        for i in range(SEQS):
-            row = q[pl.ds(b * SEQS + i, 1), :]
-            spread = jnp.where(own_head, jnp.broadcast_to(row, (heads, width)), 0.0).astype(BF16)
-            scores.append(dot(spread, k_buf[slot, i]))
-        for i in range(SEQS):
-            weights = softmax(scores[i])
-            out = lax.dot_general(weights, v_buf[slot, i], NT, preferred_element_type=F32)
-            o[pl.ds(b * SEQS + i, 1), :] = jnp.sum(jnp.where(own_head, out, 0.0), 0, keepdims=True)
-
-        @pl.when(b + SLOTS < blocks)
-        def _():
-            for c in cache_copies(b + SLOTS, slot):
-                c.start()
-
-        for n in range(SLOTS):
-            @pl.when(b == blocks - SLOTS + n)
+            key_copy(i + 1).wait()
+            value_copy(i).wait()
+        scores = scores_of(i + 1)
+        add_values(i, weights)
+        weights = softmax(scores)
+
+        @pl.when(i + 1 + SLOTS < rows)
+        def _():
+            key_copy(i + 1 + SLOTS).start()
+
+        @pl.when(i + SLOTS < rows)
+        def _():
+            value_copy(i + SLOTS).start()
+
+        for n in range(EARLY):
+            @pl.when(i == rows - 1 - EARLY + n)
             def _():
-                gate_copy(n).start()
-                up_copy(n).start()
-
-        g = lax.div(b, per_group)
-        step = lax.rem(b, per_group)
-
-        @pl.when(b == per_group - 1)
+                weight_copy(n).start()
+
+        g = lax.div(i, GROUP)
+        step = lax.rem(i, GROUP)
+
+        @pl.when(i == GROUP - 1)
         def _():
             later[1].wait()
 
-        @pl.when(step == per_group - 1)
+        @pl.when(step == GROUP - 1)
         def _():
             with jax.named_scope('project'):
                 project(g)
 
-        @pl.when((step == 0) & (b > 0))
+        @pl.when((step == 1) & (i > GROUP))
         def _():
             with jax.named_scope('pair_sum'):
                 pair_sum(g - 1)
 
-        @pl.when((step == 3) & (b > per_group))
+        @pl.when((step == 6) & (i > GROUP))
         def _():
             with jax.named_scope('finish'):
                 finish(g - 1)
 
-        return carry
-
-    lax.fori_loop(0, blocks, block, 0)
-    for n in range(SLOTS, nf):
-        gate_copy(n).start()
-        up_copy(n).start()
+        return weights
+
+    weights = lax.fori_loop(0, rows - 1, sequence, weights)
+    for n in range(EARLY, 2 * nf):
+        weight_copy(n).start()
+    with jax.named_scope('last_cache'):
+        value_copy(rows - 1).wait()
+    add_values(rows - 1, weights)
+    with jax.named_scope('project'):
+        project(groups - 1)
 
     with jax.named_scope('pair_sum'):
         pair_sum(groups - 1)
@@ -253,19 +271,17 @@
     for n in range(nd):
         down_copy(n).start()
     with jax.named_scope('norm_m'):
-        states[...] = normed(h[...].astype(F32), gm[...].astype(F32).reshape(1, d))
-
-    def gate_up(n, carry):
-        at = hidden_units(n)
+        states[0:rows, :] = normed(h[...].astype(F32), gm[...].astype(F32).reshape(1, d))
+
+    for n in range(ff // FSTEP):
+        at = pl.ds(n * FSTEP, FSTEP)
         with jax.named_scope('wait_gate_up'):
-            gate_copy(n).wait()
-            up_copy(n).wait()
-        gate = dot(states[...], wg[:, at])
-        up = dot(states[...], wu[:, at])
+            for m in range(n * FSTEP // FCHUNK, (n + 1) * FSTEP // FCHUNK):
+                gate_copy(m).wait()
+                up_copy(m).wait()
+        gate = dot(states[...], wg[:, at])[:rows]
+        up = dot(states[...], wu[:, at])[:rows]
         hid[:, at] = (gate * jax.nn.sigmoid(gate) * up).astype(BF16)
-        return carry
-
-    lax.fori_loop(0, nf, gate_up, 0)
 
     def columns(n, which):
         return pl.ds(pl.multiple_of(n * DCHUNK + which * dh, dh), dh)
@@ -281,6 +297,10 @@
 
     def copy6(n):
         return to(partner, y_ref.at[:, columns(n, core)], y_ref.at[:, columns(n, core)], s6.at[n], r6.at[n])
+
+    def out_copy(n, which, i):
+        at = columns(n, which)
+        return pltpu.make_async_copy(y_ref.at[:, at], y_hbm.at[:, at], ysem.at[i, n])
 
     def down(n):
         with jax.named_scope('wait_down'):
@@ -302,6 +322,7 @@
         total = send4[:, part(n)].astype(F32) + recv4[:, part(n)].astype(F32)
         y_ref[:, columns(n, core)] = (h[:, columns(n, core)].astype(F32) + total).astype(BF16)
         copy6(n).start()
+        out_copy(n, core, 0).start()
         return carry
 
     def down_step(n, carry):
@@ -317,7 +338,7 @@
 
     lax.fori_loop(0, nd + LAG, down_step, 0)
     lax.fori_loop(0, nd, down_finish, 0)
-    with jax.named_scope('last_waits'):
+    with jax.named_scope('send_waits'):
         for g in range(groups):
             copy1(g).wait_send()
             copy2(g).wait_send()
@@ -325,7 +346,15 @@
         for n in range(nd):
             copy4(n).wait_send()
             copy5(n).wait_send()
-            copy6(n).wait()
+    with jax.named_scope('wait_y'):
+        for n in range(nd):
+            copy6(n).wait_recv()
+            out_copy(n, other, 1).start()
+    with jax.named_scope('wait_out'):
+        for n in range(nd):
+            copy6(n).wait_send()
+            out_copy(n, core, 0).wait()
+            out_copy(n, other, 1).wait()
 
 
 def solution(mesh):
@@ -342,10 +371,10 @@
             layer_kernel,
             out_shape=jax.ShapeDtypeStruct((rows, d), BF16),
             in_specs=[pl.BlockSpec(memory_space=pl.ANY)] * 11,
-            out_specs=pl.BlockSpec(memory_space=pltpu.VMEM),
+            out_specs=pl.BlockSpec(memory_space=pl.ANY),
             scratch_shapes=[
-                pltpu.VMEM((SLOTS, SEQS, width, cache), BF16),
-                pltpu.VMEM((SLOTS, SEQS, width, cache), BF16),
+                pltpu.VMEM((SLOTS, width, cache), BF16),
+                pltpu.VMEM((SLOTS, width, cache), BF16),
                 pltpu.VMEM((d, ff), BF16),
                 pltpu.VMEM((d, ff), BF16),
                 pltpu.VMEM((ff, d), BF16),
@@ -367,11 +396,13 @@
                 pltpu.VMEM((rows, half), BF16),
                 pltpu.VMEM((rows, half), BF16),
                 pltpu.VMEM((rows, half), BF16),
+                pltpu.VMEM((PADDED, d), BF16),
+                pltpu.VMEM((rows, DCHUNK), F32),
                 pltpu.VMEM((rows, d), BF16),
-                pltpu.VMEM((rows, DCHUNK), F32),
                 dma((SLOTS,)), dma((SLOTS,)), dma((d // QCHUNK,)), dma, dma((nf,)), dma((nf,)), dma((nd,)), dma((4,)),
                 *[dma((groups,)) for _ in range(6)],
                 *[dma((nd,)) for _ in range(6)],
+                dma((2, nd)),
             ],
             compiler_params=pltpu.CompilerParams(
                 collective_id=0, has_side_effects=True, vmem_limit_bytes=67043328

time: 86.9 us -> 85.5 us (0.984)
  Pallas kernels: 85 us -> 83.6 us
    pallas_call x1, Pallas kernels: 85 us -> 83.6 us  [step(): pl.pallas_call(layer_kernel, out_shape=jax.ShapeDtypeStruct((rows, d), BF...]
where the time goes in v4:
time: 85.5 us; the launch traced here: 85.4 us
  Pallas kernels  83.6 us (98%)
  local copies, waits for them, and re-layouts  1.77 us (2%)
    pallas_call x1, Pallas kernels, step(): pl.pallas_call(layer_kernel, out_shape=jax.ShapeDtypeStruct((rows, d), BF...  83.6 us
    unnamed x1, local copies, waits for them, and re-layouts  1.77 us

profile of v4, /device:TPU:0, one launch (start us, length us, event | category | flops | bytes accessed | tf_op | source)
XLA Modules:
  0.0 85.4 jit_solution(16466969011196007650)
XLA Ops:
  0.0 83.6 %decode_layer.1 = bf16[64,3072]{1,0:T(8,128)(2,1)} custom-call(bf16[64,3072]{1,0:T(8,128)(2,1)} %x_hbm.1, bf16[64,768,1024]{2,1,0:T(8,128)(2,1)} %bitcast.1.k_hbm, bf16[64,768,1024]{2,1,0:T(8,128)(2,1)} %bitcast.3.v_hbm, bf16[3072]{0:T(1024)(128)(2,1)} %ga_hbm.1, bf16[3072,768]{1,0:T(8,128)(2,1)} %wq_hbm.1, bf16[768,3072]{1,0:T(8,128)(2,1)} %wo_hbm.1, ...), custom_call_target="tpu_custom_call" | custom-call | tf_op jit(solution)/shard_map/decode_layer/pallas_call | solution.py:370
  83.6 1.8 %copy.13 = bf16[64,3072]{1,0:T(8,128)(2,1)} copy(bf16[64,3072]{1,0:T(8,128)(2,1)} %decode_layer.1) | data formatting | bytes 786432

commit v5 on v4

--- a/solution.py
+++ b/solution.py
@@ -9,6 +9,7 @@
 HEAD = 96
 THETA = 10000
 EPS = 1e-6
+VMEM_LIMIT = 66_500_000
 EARLY = 3
 SLOTS = 5
 GROUP = 16
@@ -17,7 +18,7 @@
 FSTEP = 1024
 PADDED = 128
 DCHUNK = 512
-LAG = 2
+LAG = 1
 
 F32, BF16 = jnp.float32, jnp.bfloat16
 NT = (((1,), (1,)), ((), ()))
@@ -42,12 +43,12 @@
 
 def layer_kernel(
     x_hbm, k_hbm, v_hbm, ga_hbm, wq_hbm, wo_hbm, gm_hbm, wg_hbm, wu_hbm, wd_hbm, trig_hbm,
-    y_hbm,
+    y_ref,
     k_buf, v_buf, wg, wu, wd, wo, x, ga, gm, trig,
     q, o, term, send1, recv1, send2, recv2, h, hid,
-    send3, recv3, send4, recv4, states, piece, y_ref,
+    send3, recv3, send4, recv4, states, piece,
     ksem, vsem, qsem, wsem, gsem, usem, dsem, isem,
-    s1, r1, s2, r2, s3, r3, s4, r4, s5, r5, s6, r6, ysem,
+    s1, r1, s2, r2, s3, r3, s4, r4, s5, r5, s6, r6,
 ):
     rows, d = x.shape
     width = q.shape[1]
@@ -97,10 +98,10 @@
         return pl.ds(pl.multiple_of(n * DCHUNK, DCHUNK), DCHUNK)
 
     def gate_copy(n):
-        return pltpu.make_async_copy(wg_hbm.at[:, hidden_units(n)], wg.at[:, hidden_units(n)], gsem.at[n])
+        return pltpu.make_async_copy(wg_hbm.at[:, hidden_units(n)], wg.at[:, hidden_units(n)], gsem.at[n * FCHUNK // FSTEP])
 
     def up_copy(n):
-        return pltpu.make_async_copy(wu_hbm.at[:, hidden_units(n)], wu.at[:, hidden_units(n)], usem.at[n])
+        return pltpu.make_async_copy(wu_hbm.at[:, hidden_units(n)], wu.at[:, hidden_units(n)], usem.at[n * FCHUNK // FSTEP])
 
     def weight_copy(n):
         return (up_copy if n % 2 else gate_copy)(n // 2)
@@ -160,13 +161,13 @@
         return pl.ds(pl.multiple_of(g * GROUP, GROUP), GROUP)
 
     def copy1(g):
-        return to(partner, send1.at[rows_of(g)], recv1.at[rows_of(g)], s1.at[g], r1.at[g])
+        return to(partner, send1.at[rows_of(g)], recv1.at[rows_of(g)], s1, r1.at[g])
 
     def copy2(g):
-        return to(across, send2.at[rows_of(g)], recv2.at[rows_of(g)], s2.at[g], r2.at[g])
+        return to(across, send2.at[rows_of(g)], recv2.at[rows_of(g)], s2, r2.at[g])
 
     def copy3(g):
-        return to(partner, h.at[rows_of(g), mine], h.at[rows_of(g), mine], s3.at[g], r3.at[g])
+        return to(partner, h.at[rows_of(g), mine], h.at[rows_of(g), mine], s3, r3)
 
     def project(g):
         at = rows_of(g)
@@ -266,8 +267,7 @@
         finish(groups - 1)
     later[0].wait()
     with jax.named_scope('wait_h'):
-        for g in range(groups):
-            copy3(g).wait_recv()
+        to(partner, h.at[:, mine], h.at[:, mine], s3, r3).wait_recv()
     for n in range(nd):
         down_copy(n).start()
     with jax.named_scope('norm_m'):
@@ -276,9 +276,8 @@
     for n in range(ff // FSTEP):
         at = pl.ds(n * FSTEP, FSTEP)
         with jax.named_scope('wait_gate_up'):
-            for m in range(n * FSTEP // FCHUNK, (n + 1) * FSTEP // FCHUNK):
-                gate_copy(m).wait()
-                up_copy(m).wait()
+            pltpu.make_async_copy(wg_hbm.at[:, at], wg.at[:, at], gsem.at[n]).wait()
+            pltpu.make_async_copy(wu_hbm.at[:, at], wu.at[:, at], usem.at[n]).wait()
         gate = dot(states[...], wg[:, at])[:rows]
         up = dot(states[...], wu[:, at])[:rows]
         hid[:, at] = (gate * jax.nn.sigmoid(gate) * up).astype(BF16)
@@ -290,17 +289,13 @@
         return pl.ds(pl.multiple_of(n * dh, dh), dh)
 
     def copy4(n):
-        return to(partner, send3.at[:, part(n)], recv3.at[:, part(n)], s4.at[n], r4.at[n])
+        return to(partner, send3.at[:, part(n)], recv3.at[:, part(n)], s4, r4.at[n])
 
     def copy5(n):
-        return to(across, send4.at[:, part(n)], recv4.at[:, part(n)], s5.at[n], r5.at[n])
+        return to(across, send4.at[:, part(n)], recv4.at[:, part(n)], s5, r5.at[n])
 
     def copy6(n):
-        return to(partner, y_ref.at[:, columns(n, core)], y_ref.at[:, columns(n, core)], s6.at[n], r6.at[n])
-
-    def out_copy(n, which, i):
-        at = columns(n, which)
-        return pltpu.make_async_copy(y_ref.at[:, at], y_hbm.at[:, at], ysem.at[i, n])
+        return to(partner, y_ref.at[:, columns(n, core)], y_ref.at[:, columns(n, core)], s6, r6)
 
     def down(n):
         with jax.named_scope('wait_down'):
@@ -322,7 +317,6 @@
         total = send4[:, part(n)].astype(F32) + recv4[:, part(n)].astype(F32)
         y_ref[:, columns(n, core)] = (h[:, columns(n, core)].astype(F32) + total).astype(BF16)
         copy6(n).start()
-        out_copy(n, core, 0).start()
         return carry
 
     def down_step(n, carry):
@@ -339,22 +333,13 @@
     lax.fori_loop(0, nd + LAG, down_step, 0)
     lax.fori_loop(0, nd, down_finish, 0)
     with jax.named_scope('send_waits'):
-        for g in range(groups):
-            copy1(g).wait_send()
-            copy2(g).wait_send()
-            copy3(g).wait_send()
-        for n in range(nd):
-            copy4(n).wait_send()
-            copy5(n).wait_send()
+        for send, recv, ssem, rsem in (
+            (send1, recv1, s1, r1.at[0]), (send2, recv2, s2, r2.at[0]), (send3, recv3, s4, r4.at[0]), (send4, recv4, s5, r5.at[0]),
+        ):
+            to(partner, send, recv, ssem, rsem).wait_send()
+        to(partner, h.at[:, mine], h.at[:, mine], s3, r3).wait_send()
     with jax.named_scope('wait_y'):
-        for n in range(nd):
-            copy6(n).wait_recv()
-            out_copy(n, other, 1).start()
-    with jax.named_scope('wait_out'):
-        for n in range(nd):
-            copy6(n).wait_send()
-            out_copy(n, core, 0).wait()
-            out_copy(n, other, 1).wait()
+        to(partner, y_ref.at[:, mine], y_ref.at[:, mine], s6, r6).wait()
 
 
 def solution(mesh):
@@ -369,9 +354,9 @@
         dma = pltpu.SemaphoreType.DMA
         return pl.pallas_call(
             layer_kernel,
-            out_shape=jax.ShapeDtypeStruct((rows, d), BF16),
+            out_shape=pltpu.VMEM((rows, d), BF16),
             in_specs=[pl.BlockSpec(memory_space=pl.ANY)] * 11,
-            out_specs=pl.BlockSpec(memory_space=pl.ANY),
+            out_specs=pl.BlockSpec(memory_space=pltpu.VMEM),
             scratch_shapes=[
                 pltpu.VMEM((SLOTS, width, cache), BF16),
                 pltpu.VMEM((SLOTS, width, cache), BF16),
@@ -398,14 +383,12 @@
                 pltpu.VMEM((rows, half), BF16),
                 pltpu.VMEM((PADDED, d), BF16),
                 pltpu.VMEM((rows, DCHUNK), F32),
-                pltpu.VMEM((rows, d), BF16),
-                dma((SLOTS,)), dma((SLOTS,)), dma((d // QCHUNK,)), dma, dma((nf,)), dma((nf,)), dma((nd,)), dma((4,)),
-                *[dma((groups,)) for _ in range(6)],
-                *[dma((nd,)) for _ in range(6)],
-                dma((2, nd)),
+                dma((SLOTS,)), dma((SLOTS,)), dma((d // QCHUNK,)), dma, dma((ff // FSTEP,)), dma((ff // FSTEP,)), dma((nd,)), dma((4,)),
+                dma, dma((groups,)), dma, dma((groups,)), dma, dma,
+                dma, dma((nd,)), dma, dma((nd,)), dma, dma,
             ],
             compiler_params=pltpu.CompilerParams(
-                collective_id=0, has_side_effects=True, vmem_limit_bytes=67043328
+                collective_id=0, has_side_effects=True, vmem_limit_bytes=VMEM_LIMIT
             ),
             name="decode_layer",
         )(x, *turned_cache, gain_a, wq, wo, gain_m, w_gate, w_up, w_down, trig)

time: 85.5 us -> 83.8 us (0.980)
  local copies, waits for them, and re-layouts: 1.77 us -> 0.75 us
    unnamed x1, local copies, waits for them, and re-layouts: 1.77 us -> 0.75 us
where the time goes in v5:
time: 83.8 us; the launch traced here: 83.7 us
  Pallas kernels  82.9 us (99%)
    pallas_call x1, Pallas kernels, step(): pl.pallas_call(layer_kernel, out_shape=pltpu.VMEM((rows, d), BF16), in_sp...  82.9 us

profile of v5, /device:TPU:0, one launch (start us, length us, event | category | flops | bytes accessed | tf_op | source)
XLA Modules:
  0.0 83.7 jit_solution(13777309605573826634)
XLA Ops:
  0.0 82.9 %decode_layer.1 = bf16[64,3072]{1,0:T(8,128)(2,1)S(1)} custom-call(bf16[64,3072]{1,0:T(8,128)(2,1)} %x_hbm.1, bf16[64,768,1024]{2,1,0:T(8,128)(2,1)} %bitcast.1.k_hbm, bf16[64,768,1024]{2,1,0:T(8,128)(2,1)} %bitcast.3.v_hbm, bf16[3072]{0:T(1024)(128)(2,1)} %ga_hbm.1, bf16[3072,768]{1,0:T(8,128)(2,1)} %wq_hbm.1, bf16[768,3072]{1,0:T(8,128)(2,1)} %wo_hbm.1, ...), custom_call_target="tpu_custom_call" | custom-call | tf_op jit(solution)/shard_map/decode_layer/pallas_call | solution.py:355
  83.0 0.7 copy.13

commit v6 on v5

--- a/solution.py
+++ b/solution.py
@@ -13,10 +13,12 @@
 EARLY = 3
 SLOTS = 5
 GROUP = 16
-QCHUNK = 768
+LAST = 4
+QCHUNK = 1536
 FCHUNK = 512
-FSTEP = 1024
+FSTEPS = (1024, 512, 512)
 PADDED = 128
+DCOPY = 1024
 DCHUNK = 512
 LAG = 1
 
@@ -46,9 +48,9 @@
     y_ref,
     k_buf, v_buf, wg, wu, wd, wo, x, ga, gm, trig,
     q, o, term, send1, recv1, send2, recv2, h, hid,
-    send3, recv3, send4, recv4, states, piece,
-    ksem, vsem, qsem, wsem, gsem, usem, dsem, isem,
-    s1, r1, s2, r2, s3, r3, s4, r4, s5, r5, s6, r6,
+    send3, recv3, send4, recv4, states, piece, last_send, last_recv,
+    psem, qsem, wsem, fsem, dsem, isem,
+    sa, sb, ls, lr, r2, r3, r4, r5,
 ):
     rows, d = x.shape
     width = q.shape[1]
@@ -60,21 +62,29 @@
     other = 1 - core
     partner = t + 1 - 2 * core
     across = lax.rem(t + 2, 4)
+    diagonal = lax.rem(partner + 2, 4)
     groups = rows // GROUP
     nq, nf, nd = d // QCHUNK, ff // FCHUNK, d // DCHUNK
     dh = DCHUNK // 2
 
     barrier = pltpu.get_barrier_semaphore()
-    for peer in (partner, across):
+    for peer in (partner, across, diagonal):
         pl.semaphore_signal(barrier, inc=1, device_id={"tp": peer}, device_id_type=pl.DeviceIdType.MESH)
 
-    def key_copy(i):
+    def key_copy(i, sem):
         slot = lax.rem(i, SLOTS)
-        return pltpu.make_async_copy(k_hbm.at[i], k_buf.at[slot], ksem.at[slot])
+        return pltpu.make_async_copy(k_hbm.at[i], k_buf.at[slot], sem)
 
     def value_copy(i):
         slot = lax.rem(i, SLOTS)
-        return pltpu.make_async_copy(v_hbm.at[i], v_buf.at[slot], vsem.at[slot])
+        return pltpu.make_async_copy(v_hbm.at[i], v_buf.at[slot], psem.at[slot])
+
+    def next_key_copy(i):
+        return key_copy(i + 1, psem.at[lax.rem(i, SLOTS)])
+
+    def wait_pair(i):
+        two = pl.ds(0, 2)
+        pltpu.make_async_copy(k_hbm.at[two], k_buf.at[two], psem.at[lax.rem(i, SLOTS)]).wait()
 
     wq = wg.at[:, pl.ds(0, width)]
     first = [
@@ -91,29 +101,33 @@
         pltpu.make_async_copy(wo_hbm, wo, wsem),
     ]
 
+    step_of = [k for k, size in enumerate(FSTEPS) for _ in range(size // FCHUNK)]
+
     def hidden_units(n):
         return pl.ds(pl.multiple_of(n * FCHUNK, FCHUNK), FCHUNK)
 
-    def out_columns(n):
-        return pl.ds(pl.multiple_of(n * DCHUNK, DCHUNK), DCHUNK)
+    def out_columns(n, size):
+        return pl.ds(pl.multiple_of(n * size, size), size)
 
     def gate_copy(n):
-        return pltpu.make_async_copy(wg_hbm.at[:, hidden_units(n)], wg.at[:, hidden_units(n)], gsem.at[n * FCHUNK // FSTEP])
+        return pltpu.make_async_copy(wg_hbm.at[:, hidden_units(n)], wg.at[:, hidden_units(n)], fsem.at[step_of[n]])
 
     def up_copy(n):
-        return pltpu.make_async_copy(wu_hbm.at[:, hidden_units(n)], wu.at[:, hidden_units(n)], usem.at[n * FCHUNK // FSTEP])
+        return pltpu.make_async_copy(wu_hbm.at[:, hidden_units(n)], wu.at[:, hidden_units(n)], fsem.at[step_of[n]])
 
     def weight_copy(n):
         return (up_copy if n % 2 else gate_copy)(n // 2)
 
     def down_copy(n):
-        return pltpu.make_async_copy(wd_hbm.at[:, out_columns(n)], wd.at[:, out_columns(n)], dsem.at[n])
+        return pltpu.make_async_copy(wd_hbm.at[:, out_columns(n, DCOPY)], wd.at[:, out_columns(n, DCOPY)], dsem.at[n])
 
     for c in first + query_copy:
         c.start()
+    first_keys = key_copy(0, isem.at[4])
+    first_keys.start()
     for i in range(2):
-        key_copy(i).start()
         value_copy(i).start()
+        next_key_copy(i).start()
 
     for c in first[:3]:
         c.wait()
@@ -121,9 +135,9 @@
         a = normed(x[...].astype(F32), ga[...].astype(F32).reshape(1, d))
         states[0:rows, :] = a
         states[rows:PADDED, :] = jnp.zeros((PADDED - rows, d), BF16)
-    for i in range(2, 4):
-        key_copy(i).start()
+    for i in range(2, SLOTS - 1):
         value_copy(i).start()
+        next_key_copy(i).start()
     for n in range(nq):
         with jax.named_scope('wait_wq'):
             query_copy[n].wait()
@@ -132,9 +146,7 @@
             q[...] = part_q
         else:
             q[...] += part_q
-    for i in range(4, SLOTS):
-        key_copy(i).start()
-        value_copy(i).start()
+    value_copy(SLOTS - 1).start()
     for c in later:
         c.start()
     q0 = q[...].astype(BF16).astype(F32)
@@ -146,7 +158,8 @@
     top = lax.broadcasted_iota(jnp.int32, (heads, width), 0) * HEAD
     own_head = (lane >= top) & (lane < top + HEAD)
 
-    pl.semaphore_wait(barrier, 2)
+    o[...] = jnp.zeros_like(o)
+    pl.semaphore_wait(barrier, 3)
 
     def to(peer, src, dst, ssem, rsem):
         return pltpu.make_async_remote_copy(
@@ -154,6 +167,10 @@
             device_id={"tp": peer}, device_id_type=pl.DeviceIdType.MESH,
         )
 
+    def sent(sem):
+        three = pl.ds(0, 3 * rows // 2)
+        return to(partner, wo.at[three], wo.at[three], sem, r3)
+
     mine = pl.ds(pl.multiple_of(core * half, half), half)
     theirs = pl.ds(pl.multiple_of(other * half, half), half)
 
@@ -161,13 +178,13 @@
         return pl.ds(pl.multiple_of(g * GROUP, GROUP), GROUP)
 
     def copy1(g):
-        return to(partner, send1.at[rows_of(g)], recv1.at[rows_of(g)], s1, r1.at[g])
+        return to(partner, send1.at[rows_of(g)], recv1.at[rows_of(g)], sa, r4.at[g])
 
     def copy2(g):
-        return to(across, send2.at[rows_of(g)], recv2.at[rows_of(g)], s2, r2.at[g])
+        return to(across, send2.at[rows_of(g)], recv2.at[rows_of(g)], sa, r2.at[g])
 
     def copy3(g):
-        return to(partner, h.at[rows_of(g), mine], h.at[rows_of(g), mine], s3, r3)
+        return to(partner, h.at[rows_of(g), mine], h.at[rows_of(g), mine], sa, r3)
 
     def project(g):
         at = rows_of(g)
@@ -203,21 +220,20 @@
         out = lax.dot_general(weights, v_buf[lax.rem(i, SLOTS)], NT, preferred_element_type=F32)
         o[pl.ds(i, 1), :] = jnp.sum(jnp.where(own_head, out, 0.0), 0, keepdims=True)
 
-    key_copy(0).wait()
+    first_keys.wait()
     weights = softmax(scores_of(0))
-    key_copy(SLOTS).start()
+    next_key_copy(SLOTS - 1).start()
 
     def sequence(i, weights):
         with jax.named_scope('wait_cache'):
-            key_copy(i + 1).wait()
-            value_copy(i).wait()
+            wait_pair(i)
         scores = scores_of(i + 1)
         add_values(i, weights)
         weights = softmax(scores)
 
         @pl.when(i + 1 + SLOTS < rows)
         def _():
-            key_copy(i + 1 + SLOTS).start()
+            next_key_copy(i + SLOTS).start()
 
         @pl.when(i + SLOTS < rows)
         def _():
@@ -235,7 +251,7 @@
         def _():
             later[1].wait()
 
-        @pl.when(step == GROUP - 1)
+        @pl.when((step == GROUP - 1) | (i == rows - LAST - 1))
         def _():
             with jax.named_scope('project'):
                 project(g)
@@ -245,7 +261,12 @@
             with jax.named_scope('pair_sum'):
                 pair_sum(g - 1)
 
-        @pl.when((step == 6) & (i > GROUP))
+        @pl.when(i == rows - LAST + 1)
+        def _():
+            with jax.named_scope('pair_sum'):
+                pair_sum(groups - 1)
+
+        @pl.when((step == 8) & (i > GROUP))
         def _():
             with jax.named_scope('finish'):
                 finish(g - 1)
@@ -258,26 +279,50 @@
     with jax.named_scope('last_cache'):
         value_copy(rows - 1).wait()
     add_values(rows - 1, weights)
-    with jax.named_scope('project'):
-        project(groups - 1)
-
-    with jax.named_scope('pair_sum'):
-        pair_sum(groups - 1)
+    tail, block = pl.ds(rows - GROUP, GROUP), half // 4
+    upper = lax.broadcasted_iota(jnp.int32, (8, block), 0) < LAST
+
+    def last_copy(j, slot, peer):
+        return to(peer, last_send.at[j], last_recv.at[slot, j], ls, lr)
+
+    for j in range(2):
+        with jax.named_scope('project_last'):
+            seen = o[pl.ds(rows - 8, 8), :].astype(BF16)
+            last_term = dot(seen, wo[:, j * half:(j + 1) * half])
+            blocks = [last_term[:, k * block:(k + 1) * block] for k in range(4)]
+            packed = [jnp.where(upper, pltpu.roll(blocks[k], LAST, 0), blocks[k + 1]) for k in (0, 2)]
+            last_send[j] = jnp.concatenate(packed, 0).astype(BF16)
+            for slot, peer in ((1, across), (2, diagonal), (0, partner)):
+                last_copy(j, slot, peer).start()
     with jax.named_scope('finish'):
         finish(groups - 1)
+    with jax.named_scope('wait_h'):
+        to(partner, h.at[:, mine], h.at[:, mine], sa, r3).wait_recv()
+        sent(sa).wait_send()
     later[0].wait()
-    with jax.named_scope('wait_h'):
-        to(partner, h.at[:, mine], h.at[:, mine], s3, r3).wait_recv()
-    for n in range(nd):
+    with jax.named_scope('wait_last'):
+        to(partner, last_recv, last_recv, ls, lr).wait_recv()
+    blocks = []
+    for j in range(2):
+        near = last_send[j].astype(F32) + last_recv[0, j].astype(F32)
+        total = near + (last_recv[1, j].astype(F32) + last_recv[2, j].astype(F32))
+        for packed in (total[:8], total[8:]):
+            blocks += [pltpu.roll(packed, LAST, 0), packed]
+    last_h = x[tail, :].astype(F32)[8:] + jnp.concatenate(blocks, 1)
+    old = h[tail, :].astype(F32)
+    keep = lax.broadcasted_iota(jnp.int32, (8, d), 0) < 8 - LAST
+    h[tail, :] = jnp.concatenate([old[:8], jnp.where(keep, old[8:], last_h)], 0).astype(BF16)
+    for n in range(d // DCOPY):
         down_copy(n).start()
     with jax.named_scope('norm_m'):
         states[0:rows, :] = normed(h[...].astype(F32), gm[...].astype(F32).reshape(1, d))
 
-    for n in range(ff // FSTEP):
-        at = pl.ds(n * FSTEP, FSTEP)
+    done = 0
+    for k, size in enumerate(FSTEPS):
+        at, both = pl.ds(done, size), pl.ds(0, 2 * size)
         with jax.named_scope('wait_gate_up'):
-            pltpu.make_async_copy(wg_hbm.at[:, at], wg.at[:, at], gsem.at[n]).wait()
-            pltpu.make_async_copy(wu_hbm.at[:, at], wu.at[:, at], usem.at[n]).wait()
+            pltpu.make_async_copy(wg_hbm.at[:, both], wg.at[:, both], fsem.at[k]).wait()
+        done += size
         gate = dot(states[...], wg[:, at])[:rows]
         up = dot(states[...], wu[:, at])[:rows]
         hid[:, at] = (gate * jax.nn.sigmoid(gate) * up).astype(BF16)
@@ -289,18 +334,21 @@
         return pl.ds(pl.multiple_of(n * dh, dh), dh)
 
     def copy4(n):
-        return to(partner, send3.at[:, part(n)], recv3.at[:, part(n)], s4, r4.at[n])
+        return to(partner, send3.at[:, part(n)], recv3.at[:, part(n)], sb, r4.at[n])
 
     def copy5(n):
-        return to(across, send4.at[:, part(n)], recv4.at[:, part(n)], s5, r5.at[n])
+        return to(across, send4.at[:, part(n)], recv4.at[:, part(n)], sb, r5.at[n])
 
     def copy6(n):
-        return to(partner, y_ref.at[:, columns(n, core)], y_ref.at[:, columns(n, core)], s6, r6)
+        return to(partner, y_ref.at[:, columns(n, core)], y_ref.at[:, columns(n, core)], sb, r3)
 
     def down(n):
-        with jax.named_scope('wait_down'):
-            down_copy(n).wait()
-        piece[...] = dot(hid[...], wd[:, out_columns(n)])
+        @pl.when(lax.rem(n, DCOPY // DCHUNK) == 0)
+        def _():
+            with jax.named_scope('wait_down'):
+                down_copy(lax.div(n, DCOPY // DCHUNK)).wait()
+
+        piece[...] = dot(hid[...], wd[:, out_columns(n, DCHUNK)])
         send3[:, part(n)] = piece[:, pl.ds(pl.multiple_of(other * dh, dh), dh)].astype(BF16)
         copy4(n).start()
         term[:, part(n)] = piece[:, pl.ds(pl.multiple_of(core * dh, dh), dh)]
@@ -332,14 +380,11 @@
 
     lax.fori_loop(0, nd + LAG, down_step, 0)
     lax.fori_loop(0, nd, down_finish, 0)
+    with jax.named_scope('wait_y'):
+        to(partner, y_ref.at[:, mine], y_ref.at[:, mine], sb, r3).wait_recv()
     with jax.named_scope('send_waits'):
-        for send, recv, ssem, rsem in (
-            (send1, recv1, s1, r1.at[0]), (send2, recv2, s2, r2.at[0]), (send3, recv3, s4, r4.at[0]), (send4, recv4, s5, r5.at[0]),
-        ):
-            to(partner, send, recv, ssem, rsem).wait_send()
-        to(partner, h.at[:, mine], h.at[:, mine], s3, r3).wait_send()
-    with jax.named_scope('wait_y'):
-        to(partner, y_ref.at[:, mine], y_ref.at[:, mine], s6, r6).wait()
+        sent(sb).wait_send()
+        to(partner, last_recv, last_recv, ls, lr).wait_send()
 
 
 def solution(mesh):
@@ -383,9 +428,10 @@
                 pltpu.VMEM((rows, half), BF16),
                 pltpu.VMEM((PADDED, d), BF16),
                 pltpu.VMEM((rows, DCHUNK), F32),
-                dma((SLOTS,)), dma((SLOTS,)), dma((d // QCHUNK,)), dma, dma((ff // FSTEP,)), dma((ff // FSTEP,)), dma((nd,)), dma((4,)),
-                dma, dma((groups,)), dma, dma((groups,)), dma, dma,
-                dma, dma((nd,)), dma, dma((nd,)), dma, dma,
+                pltpu.VMEM((2, GROUP, d // 8), BF16),
+                pltpu.VMEM((3, 2, GROUP, d // 8), BF16),
+                dma((SLOTS,)), dma((d // QCHUNK,)), dma, dma((len(FSTEPS),)), dma((d // DCOPY,)), dma((5,)),
+                dma, dma, dma, dma, dma((groups,)), dma, dma((nd,)), dma((nd,)),
             ],
             compiler_params=pltpu.CompilerParams(
                 collective_id=0, has_side_effects=True, vmem_limit_bytes=VMEM_LIMIT

time: 83.8 us -> 83 us (level)
  no operation moved by 1% of the time
where the time goes in v6:
time: 83 us; the launch traced here: 82.9 us
  Pallas kernels  82.2 us (99%)
    pallas_call x1, Pallas kernels, step(): pl.pallas_call(layer_kernel, out_shape=pltpu.VMEM((rows, d), BF16), in_sp...  82.2 us

profile of v6, /device:TPU:0, one launch (start us, length us, event | category | flops | bytes accessed | tf_op | source)
XLA Modules:
  0.0 82.9 jit_solution(5156939345042314696)
XLA Ops:
  0.0 82.2 %decode_layer.1 = bf16[64,3072]{1,0:T(8,128)(2,1)S(1)} custom-call(bf16[64,3072]{1,0:T(8,128)(2,1)} %x_hbm.1, bf16[64,768,1024]{2,1,0:T(8,128)(2,1)} %bitcast.1.k_hbm, bf16[64,768,1024]{2,1,0:T(8,128)(2,1)} %bitcast.3.v_hbm, bf16[3072]{0:T(1024)(128)(2,1)} %ga_hbm.1, bf16[3072,768]{1,0:T(8,128)(2,1)} %wq_hbm.1, bf16[768,3072]{1,0:T(8,128)(2,1)} %wo_hbm.1, ...), custom_call_target="tpu_custom_call" | custom-call | tf_op jit(solution)/shard_map/decode_layer/pallas_call | solution.py:400
  82.2 0.7 copy.13
